TPU v7x, 256 devices: a 2x2x32 block of a 4x8x32 slice. The times are simulated.
256 devices in a mesh: groups: 4 (over y, x), tp: 32 (over z), sp: 2 (over core).
Axes of the slice: x: 2, y: 2, z: 32, core: 2. Of those that a mesh axis runs over, the one named last changes fastest.
The devices are a block of a 4x8x32 slice.
Arguments:
- tokens: bfloat16 [12288, 4608], P(('groups', 'tp', 'sp')), parts along dimension 0, may hold values from -48 to 48
- w_query: bfloat16 [4608, 4096], P(None, 'tp'), may hold values from -0.09375 to 0.09375
- w_key: bfloat16 [4608, 2048], P(None, 'tp'), may hold values from -0.09375 to 0.09375
- w_value: bfloat16 [4608, 2048], P(None, 'tp'), may hold values from -0.09375 to 0.09375
- w_out: bfloat16 [4096, 4608], P('tp'), may hold values from -0.5 to 0.5
- doc_lengths: int32 [32], P('groups'), parts along dimension 0, may hold values from 1 to 768, 3072 in all
Outputs:
- attn_out: bfloat16 [12288, 4608], P(('groups', 'tp', 'sp')), parts along dimension 0
There are 4 independent parts, one for each index of `groups`. A program takes and returns all parts, laid end to end along the dimension named above; an argument that names none is the same for every part. Nothing has to cross between parts.
Inputs may be any that keep to these rules, and one draw needn't show every extreme that they name: `doc_lengths`: positive lengths that sum to 3072; the largest is exactly a quarter of 3072.
All inputs are finite; a program needn't handle non-finite values.
Results may differ from a plain program's by a relative error of at most 0.024.
Values may be sent and summed in bfloat16 or wider, within the bound.
A program may use at most 128 MiB of HBM per device.

v0:
```python
import jax
import jax.numpy as jnp
from jax import lax
from jax.sharding import PartitionSpec as P

PRE_SCALE = 144


masked_low = -1e30


def partner_2(block, axis, bit):
    count = lax.axis_size(axis)
    route = []
    for low in range(count):
        high = low | 1 << bit
        if high != low and high < count:
            route += [(low, high), (high, low)]
    return lax.ppermute(block, axis, route)


def rotate(matrix, places):
    half_width = matrix.shape[1] // 2
    spread = jnp.power(
        10000.0, -(jnp.arange(half_width, dtype=jnp.float32) * (2.0 / matrix.shape[1]))
    )
    angles = places.astype(jnp.float32)[:, None] * spread[None, :]
    cosine = jnp.cos(angles)
    sine_part = jnp.sin(angles)
    lower_part = matrix[:, :half_width]
    upper_part = matrix[:, half_width:]
    return jnp.concatenate(
        [
            lower_part * cosine - upper_part * sine_part,
            upper_part * cosine + lower_part * sine_part,
        ],
        axis=1,
    )


def doc_index(places, doc_ends):
    return jnp.sum((places[:, None] >= doc_ends[None, :]).astype(jnp.int32), axis=1)


def attend(running, queries, query_places, query_docs, key_rows, value_rows, key_places, key_docs):
    query_count = queries.shape[0]
    key_count = key_rows.shape[0]
    query_block = 512
    key_block = 512
    across = key_count // key_block

    def visit_tile(step_index, carried):
        query_start = step_index // across * query_block
        key_start = step_index % across * key_block
        query_part = lax.dynamic_slice_in_dim(queries, query_start, query_block, 0)
        place_part = lax.dynamic_slice_in_dim(query_places, query_start, query_block, 0)
        docs_part = lax.dynamic_slice_in_dim(query_docs, query_start, query_block, 0)
        key_part = lax.dynamic_slice_in_dim(key_rows, key_start, key_block, 0)
        value_part = lax.dynamic_slice_in_dim(value_rows, key_start, key_block, 0)
        key_place_part = lax.dynamic_slice_in_dim(key_places, key_start, key_block, 0)
        key_docs_part = lax.dynamic_slice_in_dim(key_docs, key_start, key_block, 0)
        largest_all, denominator_all, accum_all = carried
        largest_old = lax.dynamic_slice_in_dim(largest_all, query_start, query_block, 0)
        denominator_old = lax.dynamic_slice_in_dim(denominator_all, query_start, query_block, 0)
        accum_old = lax.dynamic_slice_in_dim(accum_all, query_start, query_block, 0)
        scores = jnp.einsum("qd,kd->qk", query_part, key_part, preferred_element_type=jnp.float32)
        allowed = (key_place_part[None, :] <= place_part[:, None]) & (
            key_docs_part[None, :] == docs_part[:, None]
        )
        largest_new = jnp.maximum(
            largest_old, jnp.max(jnp.where(allowed, scores, masked_low), axis=1, keepdims=True)
        )
        weights = jnp.where(allowed, jnp.exp(scores - largest_new), 0.0)
        fading = jnp.exp(largest_old - largest_new)
        denominator_new = denominator_old * fading + jnp.sum(weights, axis=1, keepdims=True)
        accum_new = accum_old * fading + jnp.dot(
            weights.astype(jnp.bfloat16), value_part, preferred_element_type=jnp.float32
        )
        return (
            lax.dynamic_update_slice_in_dim(largest_all, largest_new, query_start, 0),
            lax.dynamic_update_slice_in_dim(denominator_all, denominator_new, query_start, 0),
            lax.dynamic_update_slice_in_dim(accum_all, accum_new, query_start, 0),
        )

    return lax.fori_loop(0, query_count // query_block * across, visit_tile, running)


def pair_up(halves, places, tp_place, half_dim):
    partner = partner_2(halves, "tp", 0)
    is_even = tp_place % 2 == 0
    lower_rows = jnp.where(is_even, halves, partner)
    upper_rows = jnp.where(is_even, partner, halves)
    key_raw = jnp.concatenate([lower_rows[:, :half_dim], upper_rows[:, :half_dim]], axis=1)
    value_rows = jnp.concatenate([lower_rows[:, half_dim:], upper_rows[:, half_dim:]], axis=1)
    key_rows = rotate(key_raw.astype(jnp.float32), places).astype(jnp.bfloat16)
    return (key_rows, value_rows)


def local(tokens, w_query, w_key, w_value, w_out, doc_lengths):
    local_rows = tokens.shape[0]
    tp_count = lax.axis_size("tp")
    sp_count = lax.axis_size("sp")
    sp_place = lax.axis_index("sp")
    tp_place = lax.axis_index("tp")
    head_dim = w_query.shape[1]
    half_dim = w_key.shape[1]
    own_rows = local_rows * tp_count
    w_input = jnp.concatenate([w_query, w_key, w_value], axis=1)
    doc_ends = jnp.cumsum(doc_lengths)
    row_ids = jnp.arange(own_rows, dtype=jnp.int32)
    query_places = (row_ids // local_rows * sp_count + sp_place) * local_rows + row_ids % local_rows
    query_docs = doc_index(query_places, doc_ends)
    produced = jnp.dot(
        lax.all_gather(tokens, "tp", axis=0, tiled=True),
        w_input,
        preferred_element_type=jnp.float32,
    )
    query_raw = produced[:, :head_dim]
    halves = produced[:, head_dim:].astype(jnp.bfloat16)
    queries = (rotate(query_raw, query_places) * PRE_SCALE ** (-0.5)).astype(jnp.bfloat16)
    key_rows, value_rows = pair_up(halves, query_places, tp_place, half_dim)
    initial = (
        jnp.full((own_rows, 1), masked_low, jnp.float32),
        jnp.zeros((own_rows, 1), jnp.float32),
        jnp.zeros((own_rows, head_dim), jnp.float32),
    )
    shard_part = (
        lax.all_gather(key_rows, "sp", axis=0, tiled=True),
        lax.all_gather(value_rows, "sp", axis=0, tiled=True),
    )
    gathered_ids = jnp.arange(shard_part[0].shape[0], dtype=jnp.int32)
    source = gathered_ids // own_rows
    within = gathered_ids % own_rows
    places = (within // local_rows * sp_count + source) * local_rows + within % local_rows
    finished = attend(
        initial,
        queries,
        query_places,
        query_docs,
        shard_part[0],
        shard_part[1],
        places,
        doc_index(places, doc_ends),
    )
    largest_all, denominator_all, accum_all = finished
    attended = (accum_all / denominator_all).astype(jnp.bfloat16)
    return lax.psum_scatter(
        jnp.dot(attended, w_out, preferred_element_type=jnp.float32).astype(jnp.bfloat16),
        "tp",
        scatter_dimension=0,
        tiled=True,
    )


def solution(mesh):
    placed = (
        P(("groups", "tp", "sp"), None),
        P(None, "tp"),
        P(None, "tp"),
        P(None, "tp"),
        P("tp", None),
        P("groups"),
    )
    return jax.shard_map(
        local,
        mesh=mesh,
        in_specs=placed,
        out_specs=P(("groups", "tp", "sp"), None),
        check_vma=False,
    )
```

profile of v0, /device:TPU:37, one launch (start us, length us, event | category | flops | bytes accessed | tf_op | source)
XLA Modules:
  0.0 510.9 jit_solution(526202389130017574)
XLA Ops:
  7.4 2.3 copy.12
  9.7 1.4 copy.13
  11.1 185.4 %all-gather.2.cloned.1.call-done = bf16[1536,4608]{1,0:T(8,128)(2,1)} async-done(((bf16[48,4608]{1,0:T(8,128)(2,1)}), bf16[1536,4608]{1,0:T(8,128)(2,1)}) %all-gather.2.cloned.1.call-update) | async-done | bytes 14155792 | tf_op jit(solution)/shard_map/all_gather | solution.py:114
  196.5 9.7 %convolution_bitcast_fusion = f32[1536,256]{0,1:T(8,128)S(1)} fusion(bf16[1536,4608]{1,0:T(8,128)(2,1)} %all-gather.2.cloned.1.call-done, bf16[4608,64]{1,0:T(8,128)(2,1)} %copy.13, bf16[4608,64]{1,0:T(8,128)(2,1)} %copy.12, bf16[4608,128]{1,0:T(8,128)(2,1)} %param.9), kind=kOutput, calls=%fused_computation.29 | convolution fusion | flops 3630956544 | bytes 18087936 | tf_op jit(solution)/shard_map/dot_general | solution.py:113
  207.0 1.3 reduce-window.8
  208.4 1.3 convert_reduce_fusion.1
  209.7 1.4 convert_reduce_fusion
  211.1 4.7 collective-permute-done
  216.0 4.2 all_gather.11
  220.3 1.7 fusion.37
  222.0 2.4 all_gather.10
  224.5 0.8 fusion.25
  225.9 96.6 %while.19 = (s32[]{:T(128)}, f32[1536,1]{0,1:T(1,128)S(1)}, f32[1536,1]{0,1:T(1,128)}, f32[1536,128]{1,0:T(8,128)S(1)}, s32[3072]{0:T(1024)}, /*index=5*/s32[153...) while((s32[]{:T(128)}, f32[1536,1]{0,1:T(1,128)S(1)}, ...), condition=%wide.region_6.7_spmd, body=%wide.region_3.6_spmd.sunk | while | flops 138806304 | bytes 4209108 | solution.py:85
  227.4 0.8 dynamic_slice.139
  228.9 1.3 select_reduce_fusion.2
  232.8 0.8 dynamic_slice.139
  234.3 1.3 select_reduce_fusion.2
  238.1 0.8 dynamic_slice.139
  239.7 1.3 select_reduce_fusion.2
  243.5 0.8 dynamic_slice.139
  245.0 1.3 select_reduce_fusion.2
  247.4 0.8 dynamic_slice.141
  248.1 0.8 dynamic_slice.142
  248.9 0.8 dynamic_slice.139
  250.4 1.3 select_reduce_fusion.2
  252.8 0.8 dynamic_slice.141
  253.5 0.8 dynamic_slice.142
  254.3 0.8 dynamic_slice.139
  255.8 1.3 select_reduce_fusion.2
  259.6 0.8 dynamic_slice.139
  261.2 1.3 select_reduce_fusion.2
  265.0 0.8 dynamic_slice.139
  266.5 1.3 select_reduce_fusion.2
  270.4 0.8 dynamic_slice.139
  271.9 1.3 select_reduce_fusion.2
  275.8 0.8 dynamic_slice.139
  277.3 1.3 select_reduce_fusion.2
  279.6 0.8 dynamic_slice.141
  280.4 0.8 dynamic_slice.142
  281.1 0.8 dynamic_slice.139
  282.7 1.3 select_reduce_fusion.2
  285.0 0.8 dynamic_slice.141
  285.8 0.8 dynamic_slice.142
  286.5 0.8 dynamic_slice.139
  288.0 1.3 select_reduce_fusion.2
  291.9 0.8 dynamic_slice.139
  293.4 1.3 select_reduce_fusion.2
  297.2 0.8 dynamic_slice.139
  298.8 1.3 select_reduce_fusion.2
  301.1 0.8 dynamic_slice.141
  302.6 0.8 dynamic_slice.139
  304.1 1.3 select_reduce_fusion.2
  308.0 0.8 dynamic_slice.139
  309.5 1.3 select_reduce_fusion.2
  311.8 0.8 dynamic_slice.141
  312.6 0.8 dynamic_slice.142
  313.4 0.8 dynamic_slice.139
  314.9 1.3 select_reduce_fusion.2
  317.2 0.8 dynamic_slice.141
  318.0 0.8 dynamic_slice.142
  318.7 0.8 dynamic_slice.139
  320.3 1.3 select_reduce_fusion.2
  323.3 7.4 %convolution_convert_fusion = bf16[1536,4608]{1,0:T(8,128)(2,1)} fusion(bf16[128,4608]{1,0:T(8,128)(2,1)S(1)} %copy-done, f32[1536,128]{1,0:T(8,128)S(1)} %get-tuple-element.273, f32[1536]{0:T(1024)S(1)} %reduce), kind=kOutput, calls=%fused_computation.28 | convolution fusion | flops 1819410432 | bytes 16128000 | tf_op jit(solution)/shard_map/dot_general | solution.py:148
  330.8 173.2 %reduce-scatter.2.cloned.1.call-done = bf16[48,4608]{1,0:T(8,128)(2,1)} async-done(((bf16[1536,4608]{1,0:T(8,128)(2,1)}), bf16[48,4608]{1,0:T(8,128)(2,1)}) %reduce-scatter.2.cloned.1.call-update) | async-done | bytes 442384 | tf_op jit(solution)/shard_map/reduce_scatter | solution.py:147
  (250 shorter events, 51.2 us)
Async XLA Ops:
  6.5 316.8 %copy-start = (bf16[128,4608]{1,0:T(8,128)(2,1)S(1)}, bf16[128,4608]{1,0:T(8,128)(2,1)}, u32[]{:S(2)}) copy-start(bf16[128,4608]{1,0:T(8,128)(2,1)} %param.12) | copy-start | bytes 3538948
  6.6 3.1 copy-start.1
  6.6 190.0 %all-gather.2.cloned.1.call-start = ((), (), s32[]{:S(2)}) async-start(), calls=%async_computation.1 | async-start | bytes 14598144 | tf_op jit(solution)/shard_map/all_gather | solution.py:114
  7.3 496.7 %reduce-scatter.2.cloned.1.call-start = ((), (), s32[]{:S(2)}) async-start(), calls=%async_computation.2 | async-start | bytes 14598144 | tf_op jit(solution)/shard_map/reduce_scatter | solution.py:147
  11.1 197.2 %copy-start.3 = (s32[1536]{0:T(1024)}, s32[1536]{0:T(1024)S(1)}, u32[]{:S(2)}) copy-start(s32[1536]{0:T(1024)S(1)} %fusion.69) | copy-start | bytes 18436
  206.3 9.5 %collective-permute-start = (bf16[1536,128]{0,1:T(8,128)(2,1)S(1)}, bf16[1536,128]{0,1:T(8,128)(2,1)S(1)}, u32[]{:S(2)}, u32[]{:S(2)}) collective-permute-start(bf16[1536,128]{0,1:T(8,128)(2,1)S(1)} %slice.58), channel_id=1, source_target_pairs={{0,2},{2,0},{4,6},{6,4},{8,10},{10,8},{12,14},{14,12},{16,18},{18,... | collective-permute-start | bytes 1179656 | tf_op jit(solution)/shard_map/ppermute | solution.py:19
  208.4 2.7 copy-start.2
  215.9 4.4 copy-start.6
  227.4 3.2 copy-start.4
  230.6 0.6 copy-start.5
  232.8 3.2 copy-start.4
  236.0 0.6 copy-start.5
  238.1 3.2 copy-start.4
  241.4 0.6 copy-start.5
  243.5 3.2 copy-start.4
  246.7 0.6 copy-start.5
  248.9 3.2 copy-start.4
  252.1 0.6 copy-start.5
  254.3 3.2 copy-start.4
  257.5 0.6 copy-start.5
  259.6 3.2 copy-start.4
  262.9 0.6 copy-start.5
  265.0 3.2 copy-start.4
  268.2 0.6 copy-start.5
  270.4 3.2 copy-start.4
  273.6 0.6 copy-start.5
  275.7 3.2 copy-start.4
  279.0 0.6 copy-start.5
  281.1 3.2 copy-start.4
  284.3 0.6 copy-start.5
  286.5 3.2 copy-start.4
  289.7 0.6 copy-start.5
  291.9 3.2 copy-start.4
  295.1 0.6 copy-start.5
  297.2 3.2 copy-start.4
  300.5 0.6 copy-start.5
  302.6 3.2 copy-start.4
  305.8 0.6 copy-start.5
  308.0 3.2 copy-start.4
  311.2 0.6 copy-start.5
  313.4 3.2 copy-start.4
  316.6 0.6 copy-start.5
  318.7 3.2 copy-start.4
  322.0 0.6 copy-start.5
Sparse Core Ops, SparseCore 0:
  9.2 187.3 all-gather.1
  330.9 173.0 reduce-scatter.1
where the time goes:
time: 514 us; the launch traced here: 511 us
  waiting for transfers between devices  364 us (71%)
  local copies, waits for them, and re-layouts  59 us (11%)
  matrix products  51 us (10%)
  other arithmetic  14.6 us (3%)
  between operations  13.6 us (3%)
  blocking collectives  6.61 us (1%)
    all_gather x1, waiting for transfers between devices, local(): lax.all_gather(tokens, 'tp', axis=0, tiled=True)  185 us
    reduce_scatter x1, waiting for transfers between devices, local(): lax.psum_scatter(jnp.dot(attended, w_out, preferred_element_type=jnp.floa...  173 us
    dot_general x18, matrix products, visit_tile(): jnp.einsum('qd,kd->qk', query_part, key_part, preferred_element_type=jnp....  23.4 us
    dynamic_slice x18, local copies, waits for them, and re-layouts, visit_tile(): lax.dynamic_slice_in_dim(query_docs, query_start, query_block, 0)  13.8 us
    dynamic_slice x18, local copies, waits for them, and re-layouts, visit_tile(): key_docs_part = lax.dynamic_slice_in_dim(key_docs, key_start, key_block, 0)  13.6 us
    dynamic_slice x18, local copies, waits for them, and re-layouts, visit_tile(): lax.dynamic_slice_in_dim(query_places, query_start, query_block, 0)  13.5 us
    dynamic_slice x18, local copies, waits for them, and re-layouts, visit_tile(): lax.dynamic_slice_in_dim(key_places, key_start, key_block, 0)  13.5 us
    dot_general x18, matrix products, visit_tile(): jnp.dot(weights.astype(jnp.bfloat16), value_part, preferred_element_type=...  10.5 us
  transfers between devices with their start and end apart: 3, of which 3 were waited for; matrix products, arithmetic and copies ran while one was open for 2% of the time, Pallas kernels for 0%

commit v1 on v0

v1 whole, which is shorter than its diff:
```python
import functools
import math

import jax
import jax.numpy as jnp
import numpy as np
from jax import lax
from jax.experimental import pallas as pl
from jax.experimental.pallas import tpu as pltpu
from jax.sharding import PartitionSpec as P

PRE_SCALE = 144
MASKED = -1e30
MESH = pl.DeviceIdType.MESH
CHUNKS = 3


def kernel(
    n, window, x_hbm, wq_hbm, wk_hbm, wv_hbm, wo_hbm, lens_ref, freq_ref, out_ref,
    tok, w_in, wk, wv, wo, cosv, sinv, query, mine, theirs, kv, att, first, acc,
    load_sem, ag_send, ag_recv, pair_send, pair_recv, sp_send, sp_recv, rs_send, rs_recv,
):
    z = lax.axis_index("tp")
    s = lax.axis_index("sp")
    right, left = lax.rem(z + 1, n), lax.rem(z + n - 1, n)
    parity = lax.rem(z, 2)
    pair = z + 1 - 2 * parity
    other = 1 - s
    side = (right, left)
    half = n // 2
    rows, depth = x_hbm.shape
    hd = wq_hbm.shape[1]
    hh = hd // 2
    sub = rows // CHUNKS
    width = depth // CHUNKS

    def block(offset):
        return lax.rem(z + offset + 2 * n, n)

    def load(src, dst, i):
        return pltpu.make_async_copy(src, dst, load_sem.at[i])

    own_load = load(x_hbm, tok.at[z], 0)
    loads = (
        load(wq_hbm, w_in.at[:, pl.ds(0, hd)], 1),
        load(wk_hbm, wk, 2),
        load(wv_hbm, wv, 3),
        load(wo_hbm, wo, 4),
    )

    def gather_copy(d, hop, b, c):
        piece = tok.at[b, pl.ds(c * sub, sub), :]
        return pltpu.make_async_remote_copy(
            src_ref=piece, dst_ref=piece,
            send_sem=ag_send.at[d, hop, c], recv_sem=ag_recv.at[d, hop, c],
            device_id={"tp": side[d]}, device_id_type=MESH,
        )

    def pair_copy(b):
        return pltpu.make_async_remote_copy(
            src_ref=mine.at[b], dst_ref=theirs.at[b],
            send_sem=pair_send.at[b], recv_sem=pair_recv.at[b],
            device_id={"tp": pair}, device_id_type=MESH,
        )

    def core_copy(b, core):
        piece = kv.at[pl.ds(pl.multiple_of((2 * b + core) * rows, 16), rows), :]
        return pltpu.make_async_remote_copy(
            src_ref=piece, dst_ref=piece,
            send_sem=sp_send.at[b], recv_sem=sp_recv.at[b],
            device_id={"sp": other}, device_id_type=MESH,
        )

    def sum_copy(d, hop, src, c):
        return pltpu.make_async_remote_copy(
            src_ref=src, dst_ref=acc.at[d, hop, c],
            send_sem=rs_send.at[d, hop, c], recv_sem=rs_recv.at[d, hop, c],
            device_id={"tp": side[d]}, device_id_type=MESH,
        )

    lane = lax.broadcasted_iota(jnp.int32, (rows, hd), 1)
    low = lane < hh
    even_mask = (lane * 0 + parity) == 0

    def turn(v, b):
        return v * cosv[b] + pltpu.roll(v, hh, 1) * sinv[b]

    def project(b):
        made = jnp.dot(tok[b], w_in[...], preferred_element_type=jnp.float32)
        places = (2 * b + s) * rows + lax.broadcasted_iota(jnp.int32, (rows, hd), 0)
        angles = places.astype(jnp.float32) * freq_ref[...]
        cosv[b] = jnp.cos(angles)
        sine = jnp.sin(angles)
        sinv[b] = jnp.where(low, -sine, sine)
        query[b] = (turn(made[:, :hd], b) * PRE_SCALE ** (-0.5)).astype(jnp.bfloat16)
        mine[b] = made[:, hd:].astype(jnp.bfloat16)

    def assemble(b):
        pair_copy(b).wait_recv()
        here = mine[b].astype(jnp.float32)
        there = theirs[b].astype(jnp.float32)
        lower = jnp.where(even_mask, here, there)
        upper = jnp.where(even_mask, there, here)
        key_raw = jnp.where(low, lower, pltpu.roll(upper, hh, 1))
        value = jnp.where(low, pltpu.roll(lower, hh, 1), upper)
        at = pl.ds(pl.multiple_of((2 * b + s) * rows, 16), rows)
        kv[at, pl.ds(0, hd)] = turn(key_raw, b).astype(jnp.bfloat16)
        kv[at, pl.ds(hd, hd)] = value.astype(jnp.bfloat16)

    def attend(b, slot):
        start = pl.multiple_of(jnp.maximum((2 * b + s + 1) * rows - window, 0), 16)
        keys = kv[pl.ds(start, window), pl.ds(0, hd)]
        values = kv[pl.ds(start, window), pl.ds(hd, hd)]
        scores = lax.dot_general(
            query[b], keys, (((1,), (1,)), ((), ())), preferred_element_type=jnp.float32
        )
        place = (2 * b + s) * rows + lax.broadcasted_iota(jnp.int32, (rows, 1), 0)
        opens = jnp.zeros((rows, 1), jnp.int32)
        end = jnp.int32(0)
        for j in range(lens_ref.shape[0]):
            end = end + lens_ref[j]
            opens = jnp.where(place >= end, end, opens)
        key_place = start + lax.broadcasted_iota(jnp.int32, (rows, window), 1)
        allowed = (key_place <= place) & (key_place >= opens)
        masked = jnp.where(allowed, scores, MASKED)
        largest = jnp.max(masked, axis=1, keepdims=True)
        weights = jnp.where(allowed, jnp.exp(masked - largest), 0.0)
        denominator = jnp.sum(weights, axis=1, keepdims=True)
        mixed = jnp.dot(
            weights.astype(jnp.bfloat16), values, preferred_element_type=jnp.float32
        )
        att[slot] = (mixed / denominator).astype(jnp.bfloat16)

    def partial(slot, c):
        return jnp.dot(
            att[slot], wo[:, pl.ds(c * width, width)], preferred_element_type=jnp.float32
        )

    own_load.start()
    for copy in loads:
        copy.start()
    barrier = pltpu.get_barrier_semaphore()
    for where in ({"tp": left}, {"tp": right}, {"sp": other}):
        pl.semaphore_signal(barrier, inc=1, device_id=where, device_id_type=MESH)
    pl.semaphore_wait(barrier, 3)
    own_load.wait()
    for c in range(CHUNKS):
        for d in range(2):
            gather_copy(d, 0, z, c).start()
    for copy in loads:
        copy.wait()
    w_in[:, pl.ds(hd, hd)] = jnp.concatenate([wk[...], wv[...]], axis=1)
    project(z)
    pair_copy(z).start()

    def gather_step(t, _):
        came = (block(-1 - t), block(1 + t))
        for c in range(CHUNKS):
            for d in range(2):
                gather_copy(d, t, came[d], c).wait_recv()

                @pl.when((t < half - 2) | (parity == 1 - d))
                def _():
                    gather_copy(d, t + 1, came[d], c).start()

            if c == 0:

                @pl.when(t == 1)
                def _():
                    assemble(z)
                    core_copy(z, s).start()

                @pl.when(t >= 2)
                def _():
                    for b in (block(1 - t), block(t - 1)):
                        assemble(b)
                        core_copy(b, s).start()

        for b in came:
            project(b)
            pair_copy(b).start()
        return 0

    lax.fori_loop(0, half - 1, gather_step, 0)
    far = block(half)
    late = (block(2 - half), block(half - 2), block(1 - half), block(half - 1), far)
    for b in late[:2]:
        assemble(b)
        core_copy(b, s).start()
    for c in range(CHUNKS):
        for d in range(2):

            @pl.when(parity == d)
            def _():
                gather_copy(d, half - 1, far, c).wait_recv()

    project(far)
    pair_copy(far).start()
    for b in late[2:]:
        assemble(b)
        core_copy(b, s).start()

    def core_arrival(b, _):
        core_copy(b, other).wait_recv()
        return 0

    lax.fori_loop(0, n, core_arrival, 0)

    attend(far, 0)
    for c in range(CHUNKS):
        first[c] = partial(0, c).astype(jnp.bfloat16)
        for d in range(2):

            @pl.when(s == d)
            def _():
                sum_copy(d, 0, first.at[c], c).start()

    attend(block(half - 1), 0)
    attend(block(1 - half), 1)

    def sum_step(t, _):
        for c in range(CHUNKS):
            for d in range(2):
                term = partial(d, c)
                here = acc.at[d, t - 1, c]
                arrives = (t > 1) | (s == d)

                @pl.when(arrives)
                def _():
                    sum_copy(d, t - 1, here, c).wait_recv()
                    here[...] = (here[...].astype(jnp.float32) + term).astype(jnp.bfloat16)

                @pl.when(jnp.logical_not(arrives))
                def _():
                    here[...] = term.astype(jnp.bfloat16)

                sum_copy(d, t, here, c).start()
        attend(block(half - 1 - t), 0)
        attend(block(t + 1 - half), 1)
        return 0

    lax.fori_loop(1, half, sum_step, 0)
    for c in range(CHUNKS):
        term = partial(0, c)
        for d in range(2):
            sum_copy(d, half - 1, acc.at[d, half - 1, c], c).wait_recv()
            term = term + acc[d, half - 1, c].astype(jnp.float32)
        out_ref[:, pl.ds(c * width, width)] = term.astype(jnp.bfloat16)

    def sends_done(t, _):
        for c in range(CHUNKS):
            for d in range(2):

                @pl.when((t < half - 1) | (lax.rem(z + half - 1, 2) == d))
                def _():
                    gather_copy(d, t, z, c).wait_send()

                @pl.when((t > 0) | (s == d))
                def _():
                    sum_copy(d, t, first.at[c], c).wait_send()

        return 0

    lax.fori_loop(0, half, sends_done, 0)

    def block_sends_done(b, _):
        pair_copy(b).wait_send()
        core_copy(b, s).wait_send()
        return 0

    lax.fori_loop(0, n, block_sends_done, 0)


def layer(n, cores, tokens, w_query, w_key, w_value, w_out, doc_lengths):
    rows, depth = tokens.shape
    hd = w_query.shape[1]
    half = n // 2
    total = n * cores * rows
    longest = total // 4
    window = min(-(-(longest + rows) // 128) * 128, total)
    width = depth // CHUNKS
    spread = np.power(
        np.float32(10000.0), -(np.arange(hd // 2, dtype=np.float32) * np.float32(2.0 / hd))
    ).astype(np.float32)
    freq = jnp.asarray(np.concatenate([spread, spread])[None, :])
    anywhere = pl.BlockSpec(memory_space=pl.ANY)
    vmem = pl.BlockSpec(memory_space=pltpu.VMEM)
    bf16, f32, dma = jnp.bfloat16, jnp.float32, pltpu.SemaphoreType.DMA
    return pl.pallas_call(
        functools.partial(kernel, n, window),
        out_shape=jax.ShapeDtypeStruct((rows, depth), bf16),
        in_specs=[anywhere] * 5 + [pl.BlockSpec(memory_space=pltpu.SMEM), vmem],
        out_specs=vmem,
        scratch_shapes=[
            pltpu.VMEM((n, rows, depth), bf16),
            pltpu.VMEM((depth, 2 * hd), bf16),
            pltpu.VMEM((depth, hd // 2), bf16),
            pltpu.VMEM((depth, hd // 2), bf16),
            pltpu.VMEM((hd, depth), bf16),
            pltpu.VMEM((n, rows, hd), f32),
            pltpu.VMEM((n, rows, hd), f32),
            pltpu.VMEM((n, rows, hd), bf16),
            pltpu.VMEM((n, rows, hd), bf16),
            pltpu.VMEM((n, rows, hd), bf16),
            pltpu.VMEM((total, 2 * hd), bf16),
            pltpu.VMEM((2, rows, hd), bf16),
            pltpu.VMEM((CHUNKS, rows, width), bf16),
            pltpu.VMEM((2, half, CHUNKS, rows, width), bf16),
            dma((5,)),
            dma((2, half, CHUNKS)),
            dma((2, half, CHUNKS)),
            dma((n,)),
            dma((n,)),
            dma((n,)),
            dma((n,)),
            dma((2, half, CHUNKS)),
            dma((2, half, CHUNKS)),
        ],
        compiler_params=pltpu.CompilerParams(
            collective_id=0, has_side_effects=True, vmem_limit_bytes=60 * 1024 * 1024
        ),
    )(tokens, w_query, w_key, w_value, w_out, doc_lengths, freq)


def solution(mesh):
    placed = (
        P(("groups", "tp", "sp"), None),
        P(None, "tp"),
        P(None, "tp"),
        P(None, "tp"),
        P("tp", None),
        P("groups"),
    )
    return jax.shard_map(
        functools.partial(layer, mesh.shape["tp"], mesh.shape["sp"]),
        mesh=mesh,
        in_specs=placed,
        out_specs=P(("groups", "tp", "sp"), None),
        check_vma=False,
    )
```

time: 514 us -> 350 us (0.68)
  waiting for transfers between devices: 364 us -> 0 us
  Pallas kernels: 0 us -> 344 us
  local copies, waits for them, and re-layouts: 59 us -> 5.54 us
  matrix products: 51 us -> 0 us
  other arithmetic: 14.6 us -> 0 us
  between operations: 13.6 us -> 0.01 us
  blocking collectives: 6.61 us -> 0 us
    pallas_call x0 -> x1, Pallas kernels: none -> 344 us  [layer(): pl.pallas_call(functools.partial(kernel, n, window), out_shape=jax.ShapeD...]
    all_gather x1 -> x0, waiting for transfers between devices: 185 us -> none  [local(): lax.all_gather(tokens, 'tp', axis=0, tiled=True)]
    reduce_scatter x1 -> x0, waiting for transfers between devices: 173 us -> none  [local(): lax.psum_scatter(jnp.dot(attended, w_out, preferred_element_type=jnp.floa...]
    dynamic_slice x72 -> x0, local copies, waits for them, and re-layouts: 54.3 us -> none  [the longest x18 13.8 us: visit_tile(): lax.dynamic_slice_in_dim(query_docs, query_start, query_block, 0)]
    dot_general x38 -> x0, matrix products: 51 us -> none  [the longest x18 23.4 us: visit_tile(): jnp.einsum('qd,kd->qk', query_part, key_part, preferred_element_type=jnp....]
    reduce_sum x20 -> x0, other arithmetic: 8.42 us -> none  [the longest x18 5.73 us: visit_tile(): jnp.sum(weights, axis=1, keepdims=True)]
    all_gather x2 -> x0, blocking collectives: 6.61 us -> none  [the longest x1 4.19 us: local(): lax.all_gather(value_rows, 'sp', axis=0, tiled=True)]
  transfers between devices with their start and end apart: 3 -> 0, of which waited for: 3 -> 0; matrix products, arithmetic and copies ran while one was open for 2% -> 0% of each run, Pallas kernels for 0% -> 0%
where the time goes in v1:
time: 350 us
  Pallas kernels  344 us (98%)
  local copies, waits for them, and re-layouts  5.54 us (2%)
    pallas_call x1, Pallas kernels, layer(): pl.pallas_call(functools.partial(kernel, n, window), out_shape=jax.ShapeD...  344 us

profile of v1, /device:TPU:37, one launch (start us, length us, event | category | flops | bytes accessed | tf_op | source)
XLA Modules:
  0.0 349.7 jit_solution(3042382803626532509)
XLA Ops:
  0.0 0.0 copy-start
  0.0 2.3 copy.8.wk_hbm
  2.3 0.0 copy-done
  2.3 1.4 copy.9.wv_hbm
  3.7 344.2 %shard_map.73 = bf16[48,4608]{1,0:T(8,128)(2,1)} custom-call(bf16[48,4608]{1,0:T(8,128)(2,1)} %x_hbm.1, bf16[4608,128]{1,0:T(8,128)(2,1)} %wq_hbm.1, bf16[4608,64]{1,0:T(8,128)(2,1)} %copy.8.wk_hbm, bf16[4608,64]{1,0:T(8,128)(2,1)} %copy.9.wv_hbm, bf16[128,4608]{1,0:T(8,128)(2,1)} %wo_hbm.1, s32[8]{0:T(128)} %lens_ref.1, f32[1,128]{1,0:T(1,128)} %constant.2.clone.freq_ref), custom_call_target="tpu_custom_call" | custom-call | tf_op jit(solution)/shard_map/pallas_call | solution.py:289
  347.9 1.8 copy.11
Async XLA Ops:
  0.0 2.3 copy-start

commit v2 on v1

--- a/solution.py
+++ b/solution.py
@@ -13,11 +13,12 @@
 MASKED = -1e30
 MESH = pl.DeviceIdType.MESH
 CHUNKS = 3
+LAG = 4
 
 
 def kernel(
     n, window, x_hbm, wq_hbm, wk_hbm, wv_hbm, wo_hbm, lens_ref, freq_ref, out_ref,
-    tok, w_in, wk, wv, wo, cosv, sinv, query, mine, theirs, kv, att, first, acc,
+    tok, wq, w_kv, wo, cosv, sinv, query, mine, theirs, kv, att, first, acc,
     load_sem, ag_send, ag_recv, pair_send, pair_recv, sp_send, sp_recv, rs_send, rs_recv,
 ):
     z = lax.axis_index("tp")
@@ -28,6 +29,7 @@
     other = 1 - s
     side = (right, left)
     half = n // 2
+    lag = min(LAG, half - 1)
     rows, depth = x_hbm.shape
     hd = wq_hbm.shape[1]
     hh = hd // 2
@@ -42,9 +44,9 @@
 
     own_load = load(x_hbm, tok.at[z], 0)
     loads = (
-        load(wq_hbm, w_in.at[:, pl.ds(0, hd)], 1),
-        load(wk_hbm, wk, 2),
-        load(wv_hbm, wv, 3),
+        load(wq_hbm, wq, 1),
+        load(wk_hbm, w_kv.at[pl.ds(0, hh), :], 2),
+        load(wv_hbm, w_kv.at[pl.ds(hh, hh), :], 3),
         load(wo_hbm, wo, 4),
     )
 
@@ -86,14 +88,17 @@
         return v * cosv[b] + pltpu.roll(v, hh, 1) * sinv[b]
 
     def project(b):
-        made = jnp.dot(tok[b], w_in[...], preferred_element_type=jnp.float32)
+        made = jnp.dot(tok[b], wq[...], preferred_element_type=jnp.float32)
+        shared = lax.dot_general(
+            tok[b], w_kv[...], (((1,), (1,)), ((), ())), preferred_element_type=jnp.float32
+        )
         places = (2 * b + s) * rows + lax.broadcasted_iota(jnp.int32, (rows, hd), 0)
         angles = places.astype(jnp.float32) * freq_ref[...]
         cosv[b] = jnp.cos(angles)
         sine = jnp.sin(angles)
         sinv[b] = jnp.where(low, -sine, sine)
-        query[b] = (turn(made[:, :hd], b) * PRE_SCALE ** (-0.5)).astype(jnp.bfloat16)
-        mine[b] = made[:, hd:].astype(jnp.bfloat16)
+        query[b] = (turn(made, b) * PRE_SCALE ** (-0.5)).astype(jnp.bfloat16)
+        mine[b] = shared.astype(jnp.bfloat16)
 
     def assemble(b):
         pair_copy(b).wait_recv()
@@ -106,6 +111,7 @@
         at = pl.ds(pl.multiple_of((2 * b + s) * rows, 16), rows)
         kv[at, pl.ds(0, hd)] = turn(key_raw, b).astype(jnp.bfloat16)
         kv[at, pl.ds(hd, hd)] = value.astype(jnp.bfloat16)
+        core_copy(b, s).start()
 
     def attend(b, slot):
         start = pl.multiple_of(jnp.maximum((2 * b + s + 1) * rows - window, 0), 16)
@@ -149,7 +155,6 @@
             gather_copy(d, 0, z, c).start()
     for copy in loads:
         copy.wait()
-    w_in[:, pl.ds(hd, hd)] = jnp.concatenate([wk[...], wv[...]], axis=1)
     project(z)
     pair_copy(z).start()
 
@@ -165,16 +170,14 @@
 
             if c == 0:
 
-                @pl.when(t == 1)
+                @pl.when(t == lag - 1)
                 def _():
                     assemble(z)
-                    core_copy(z, s).start()
-
-                @pl.when(t >= 2)
-                def _():
-                    for b in (block(1 - t), block(t - 1)):
-                        assemble(b)
-                        core_copy(b, s).start()
+
+                @pl.when(t >= lag)
+                def _():
+                    assemble(block(lag - 1 - t))
+                    assemble(block(t + 1 - lag))
 
         for b in came:
             project(b)
@@ -183,10 +186,9 @@
 
     lax.fori_loop(0, half - 1, gather_step, 0)
     far = block(half)
-    late = (block(2 - half), block(half - 2), block(1 - half), block(half - 1), far)
-    for b in late[:2]:
-        assemble(b)
-        core_copy(b, s).start()
+    for u in range(half - 1 - lag, half - 2):
+        assemble(block(-1 - u))
+        assemble(block(1 + u))
     for c in range(CHUNKS):
         for d in range(2):
 
@@ -196,9 +198,8 @@
 
     project(far)
     pair_copy(far).start()
-    for b in late[2:]:
+    for b in (far, block(half - 1), block(1 - half)):
         assemble(b)
-        core_copy(b, s).start()
 
     def core_arrival(b, _):
         core_copy(b, other).wait_recv()
@@ -237,6 +238,17 @@
                 sum_copy(d, t, here, c).start()
         attend(block(half - 1 - t), 0)
         attend(block(t + 1 - half), 1)
+        for b in (2 * t, 2 * t + 1):
+            pair_copy(b).wait_send()
+            core_copy(b, s).wait_send()
+        for c in range(CHUNKS):
+            for d in range(2):
+                gather_copy(d, t - 1, z, c).wait_send()
+
+                @pl.when((t > 2) | ((t == 2) & (s == d)))
+                def _():
+                    sum_copy(d, t - 2, first.at[c], c).wait_send()
+
         return 0
 
     lax.fori_loop(1, half, sum_step, 0)
@@ -247,28 +259,18 @@
             term = term + acc[d, half - 1, c].astype(jnp.float32)
         out_ref[:, pl.ds(c * width, width)] = term.astype(jnp.bfloat16)
 
-    def sends_done(t, _):
-        for c in range(CHUNKS):
-            for d in range(2):
-
-                @pl.when((t < half - 1) | (lax.rem(z + half - 1, 2) == d))
-                def _():
-                    gather_copy(d, t, z, c).wait_send()
-
-                @pl.when((t > 0) | (s == d))
-                def _():
-                    sum_copy(d, t, first.at[c], c).wait_send()
-
-        return 0
-
-    lax.fori_loop(0, half, sends_done, 0)
-
-    def block_sends_done(b, _):
+    for b in range(2):
         pair_copy(b).wait_send()
         core_copy(b, s).wait_send()
-        return 0
-
-    lax.fori_loop(0, n, block_sends_done, 0)
+    for c in range(CHUNKS):
+        for d in range(2):
+
+            @pl.when(parity == 1 - d)
+            def _():
+                gather_copy(d, half - 1, z, c).wait_send()
+
+            for hop in (half - 2, half - 1):
+                sum_copy(d, hop, first.at[c], c).wait_send()
 
 
 def layer(n, cores, tokens, w_query, w_key, w_value, w_out, doc_lengths):
@@ -293,9 +295,8 @@
         out_specs=vmem,
         scratch_shapes=[
             pltpu.VMEM((n, rows, depth), bf16),
-            pltpu.VMEM((depth, 2 * hd), bf16),
-            pltpu.VMEM((depth, hd // 2), bf16),
-            pltpu.VMEM((depth, hd // 2), bf16),
+            pltpu.VMEM((depth, hd), bf16),
+            pltpu.VMEM((hd, depth), bf16),
             pltpu.VMEM((hd, depth), bf16),
             pltpu.VMEM((n, rows, hd), f32),
             pltpu.VMEM((n, rows, hd), f32),
@@ -319,7 +320,7 @@
         compiler_params=pltpu.CompilerParams(
             collective_id=0, has_side_effects=True, vmem_limit_bytes=60 * 1024 * 1024
         ),
-    )(tokens, w_query, w_key, w_value, w_out, doc_lengths, freq)
+    )(tokens, w_query, w_key.T, w_value.T, w_out, doc_lengths, freq)
 
 
 def solution(mesh):

time: 350 us -> 343 us (0.980)
  local copies, waits for them, and re-layouts: 5.54 us -> 1.8 us
    unnamed x5 -> x1, local copies, waits for them, and re-layouts: 5.54 us -> 1.8 us
where the time goes in v2:
time: 343 us
  Pallas kernels  341 us (99%)
    pallas_call x1, Pallas kernels, layer(): pl.pallas_call(functools.partial(kernel, n, window), out_shape=jax.ShapeD...  341 us

profile of v2, /device:TPU:37, one launch (start us, length us, event | category | flops | bytes accessed | tf_op | source)
XLA Modules:
  0.0 342.7 jit_solution(8074047137913625485)
XLA Ops:
  0.0 340.9 %shard_map.73 = bf16[48,4608]{1,0:T(8,128)(2,1)} custom-call(bf16[48,4608]{1,0:T(8,128)(2,1)} %x_hbm.1, bf16[4608,128]{1,0:T(8,128)(2,1)} %wq_hbm.1, bf16[64,4608]{1,0:T(8,128)(2,1)} %bitcast.2, bf16[64,4608]{1,0:T(8,128)(2,1)} %bitcast.3, bf16[128,4608]{1,0:T(8,128)(2,1)} %wo_hbm.1, s32[8]{0:T(128)} %lens_ref.1, f32[1,128]{1,0:T(1,128)} %constant.2.clone.freq_ref), custom_call_target="tpu_custom_call" | custom-call | tf_op jit(solution)/shard_map/pallas_call | solution.py:291
  340.9 1.8 copy.9

commit v3 on v2

--- a/solution.py
+++ b/solution.py
@@ -54,14 +54,14 @@
         piece = tok.at[b, pl.ds(c * sub, sub), :]
         return pltpu.make_async_remote_copy(
             src_ref=piece, dst_ref=piece,
-            send_sem=ag_send.at[d, hop, c], recv_sem=ag_recv.at[d, hop, c],
+            send_sem=ag_send.at[0], recv_sem=ag_recv.at[d, hop, c],
             device_id={"tp": side[d]}, device_id_type=MESH,
         )
 
     def pair_copy(b):
         return pltpu.make_async_remote_copy(
             src_ref=mine.at[b], dst_ref=theirs.at[b],
-            send_sem=pair_send.at[b], recv_sem=pair_recv.at[b],
+            send_sem=pair_send.at[0], recv_sem=pair_recv.at[b],
             device_id={"tp": pair}, device_id_type=MESH,
         )
 
@@ -69,15 +69,21 @@
         piece = kv.at[pl.ds(pl.multiple_of((2 * b + core) * rows, 16), rows), :]
         return pltpu.make_async_remote_copy(
             src_ref=piece, dst_ref=piece,
-            send_sem=sp_send.at[b], recv_sem=sp_recv.at[b],
+            send_sem=sp_send.at[0], recv_sem=sp_recv.at[0],
             device_id={"sp": other}, device_id_type=MESH,
         )
 
-    def sum_copy(d, hop, src, c):
+    def sum_copy(d, hop, src, c, stage=1):
         return pltpu.make_async_remote_copy(
             src_ref=src, dst_ref=acc.at[d, hop, c],
-            send_sem=rs_send.at[d, hop, c], recv_sem=rs_recv.at[d, hop, c],
+            send_sem=rs_send.at[stage], recv_sem=rs_recv.at[d, hop, c],
             device_id={"tp": side[d]}, device_id_type=MESH,
+        )
+
+    def whole(ref, send, recv, where):
+        return pltpu.make_async_remote_copy(
+            src_ref=ref, dst_ref=ref, send_sem=send, recv_sem=recv,
+            device_id=where, device_id_type=MESH,
         )
 
     lane = lax.broadcasted_iota(jnp.int32, (rows, hd), 1)
@@ -88,17 +94,18 @@
         return v * cosv[b] + pltpu.roll(v, hh, 1) * sinv[b]
 
     def project(b):
-        made = jnp.dot(tok[b], wq[...], preferred_element_type=jnp.float32)
         shared = lax.dot_general(
             tok[b], w_kv[...], (((1,), (1,)), ((), ())), preferred_element_type=jnp.float32
         )
+        mine[b] = shared.astype(jnp.bfloat16)
+        pair_copy(b).start()
+        made = jnp.dot(tok[b], wq[...], preferred_element_type=jnp.float32)
         places = (2 * b + s) * rows + lax.broadcasted_iota(jnp.int32, (rows, hd), 0)
         angles = places.astype(jnp.float32) * freq_ref[...]
         cosv[b] = jnp.cos(angles)
         sine = jnp.sin(angles)
         sinv[b] = jnp.where(low, -sine, sine)
         query[b] = (turn(made, b) * PRE_SCALE ** (-0.5)).astype(jnp.bfloat16)
-        mine[b] = shared.astype(jnp.bfloat16)
 
     def assemble(b):
         pair_copy(b).wait_recv()
@@ -156,7 +163,6 @@
     for copy in loads:
         copy.wait()
     project(z)
-    pair_copy(z).start()
 
     def gather_step(t, _):
         came = (block(-1 - t), block(1 + t))
@@ -181,7 +187,6 @@
 
         for b in came:
             project(b)
-            pair_copy(b).start()
         return 0
 
     lax.fori_loop(0, half - 1, gather_step, 0)
@@ -189,6 +194,7 @@
     for u in range(half - 1 - lag, half - 2):
         assemble(block(-1 - u))
         assemble(block(1 + u))
+    assemble(block((1 - 2 * parity) * (half - 1)))
     for c in range(CHUNKS):
         for d in range(2):
 
@@ -197,15 +203,10 @@
                 gather_copy(d, half - 1, far, c).wait_recv()
 
     project(far)
-    pair_copy(far).start()
-    for b in (far, block(half - 1), block(1 - half)):
-        assemble(b)
-
-    def core_arrival(b, _):
-        core_copy(b, other).wait_recv()
-        return 0
-
-    lax.fori_loop(0, n, core_arrival, 0)
+    assemble(far)
+    assemble(block((2 * parity - 1) * (half - 1)))
+    cores_kv = whole(kv.at[pl.ds(0, n * rows), :], sp_send.at[0], sp_recv.at[0], {"sp": other})
+    cores_kv.wait_recv()
 
     attend(far, 0)
     for c in range(CHUNKS):
@@ -214,7 +215,7 @@
 
             @pl.when(s == d)
             def _():
-                sum_copy(d, 0, first.at[c], c).start()
+                sum_copy(d, 0, first.at[c], c, 0).start()
 
     attend(block(half - 1), 0)
     attend(block(1 - half), 1)
@@ -238,17 +239,6 @@
                 sum_copy(d, t, here, c).start()
         attend(block(half - 1 - t), 0)
         attend(block(t + 1 - half), 1)
-        for b in (2 * t, 2 * t + 1):
-            pair_copy(b).wait_send()
-            core_copy(b, s).wait_send()
-        for c in range(CHUNKS):
-            for d in range(2):
-                gather_copy(d, t - 1, z, c).wait_send()
-
-                @pl.when((t > 2) | ((t == 2) & (s == d)))
-                def _():
-                    sum_copy(d, t - 2, first.at[c], c).wait_send()
-
         return 0
 
     lax.fori_loop(1, half, sum_step, 0)
@@ -259,18 +249,12 @@
             term = term + acc[d, half - 1, c].astype(jnp.float32)
         out_ref[:, pl.ds(c * width, width)] = term.astype(jnp.bfloat16)
 
-    for b in range(2):
-        pair_copy(b).wait_send()
-        core_copy(b, s).wait_send()
-    for c in range(CHUNKS):
-        for d in range(2):
-
-            @pl.when(parity == 1 - d)
-            def _():
-                gather_copy(d, half - 1, z, c).wait_send()
-
-            for hop in (half - 2, half - 1):
-                sum_copy(d, hop, first.at[c], c).wait_send()
+    cores_kv.wait_send()
+    ring = {"tp": right}
+    whole(mine, pair_send.at[0], pair_recv.at[0], ring).wait_send()
+    whole(tok.at[pl.ds(0, n - 1)], ag_send.at[0], ag_recv.at[0, 0, 0], ring).wait_send()
+    whole(first, rs_send.at[0], rs_recv.at[0, 0, 0], ring).wait_send()
+    whole(acc.at[:, pl.ds(0, half - 1)], rs_send.at[1], rs_recv.at[0, 0, 0], ring).wait_send()
 
 
 def layer(n, cores, tokens, w_query, w_key, w_value, w_out, doc_lengths):
@@ -308,13 +292,13 @@
             pltpu.VMEM((CHUNKS, rows, width), bf16),
             pltpu.VMEM((2, half, CHUNKS, rows, width), bf16),
             dma((5,)),
+            dma((1,)),
             dma((2, half, CHUNKS)),
-            dma((2, half, CHUNKS)),
+            dma((1,)),
             dma((n,)),
-            dma((n,)),
-            dma((n,)),
-            dma((n,)),
-            dma((2, half, CHUNKS)),
+            dma((1,)),
+            dma((1,)),
+            dma((2,)),
             dma((2, half, CHUNKS)),
         ],
         compiler_params=pltpu.CompilerParams(

time: 343 us -> 340 us (level)
  no operation moved by 1% of the time
where the time goes in v3:
time: 340 us
  Pallas kernels  338 us (99%)
    pallas_call x1, Pallas kernels, layer(): pl.pallas_call(functools.partial(kernel, n, window), out_shape=jax.ShapeD...  338 us

profile of v3, /device:TPU:37, one launch (start us, length us, event | category | flops | bytes accessed | tf_op | source)
XLA Modules:
  0.0 339.7 jit_solution(16893479303707917512)
XLA Ops:
  0.0 337.8 %shard_map.73 = bf16[48,4608]{1,0:T(8,128)(2,1)} custom-call(bf16[48,4608]{1,0:T(8,128)(2,1)} %x_hbm.1, bf16[4608,128]{1,0:T(8,128)(2,1)} %wq_hbm.1, bf16[64,4608]{1,0:T(8,128)(2,1)} %bitcast.2, bf16[64,4608]{1,0:T(8,128)(2,1)} %bitcast.3, bf16[128,4608]{1,0:T(8,128)(2,1)} %wo_hbm.1, s32[8]{0:T(128)} %lens_ref.1, f32[1,128]{1,0:T(1,128)} %constant.2.clone.freq_ref), custom_call_target="tpu_custom_call" | custom-call | tf_op jit(solution)/shard_map/pallas_call | solution.py:275
  337.9 1.8 copy.9

commit v4 on v3

--- a/solution.py
+++ b/solution.py
@@ -13,7 +13,7 @@
 MASKED = -1e30
 MESH = pl.DeviceIdType.MESH
 CHUNKS = 3
-LAG = 4
+SLOTS = 4
 
 
 def kernel(
@@ -29,7 +29,6 @@
     other = 1 - s
     side = (right, left)
     half = n // 2
-    lag = min(LAG, half - 1)
     rows, depth = x_hbm.shape
     hd = wq_hbm.shape[1]
     hh = hd // 2
@@ -54,7 +53,7 @@
         piece = tok.at[b, pl.ds(c * sub, sub), :]
         return pltpu.make_async_remote_copy(
             src_ref=piece, dst_ref=piece,
-            send_sem=ag_send.at[0], recv_sem=ag_recv.at[d, hop, c],
+            send_sem=ag_send.at[0], recv_sem=ag_recv.at[d, lax.rem(hop, SLOTS), c],
             device_id={"tp": side[d]}, device_id_type=MESH,
         )
 
@@ -76,7 +75,7 @@
     def sum_copy(d, hop, src, c, stage=1):
         return pltpu.make_async_remote_copy(
             src_ref=src, dst_ref=acc.at[d, hop, c],
-            send_sem=rs_send.at[stage], recv_sem=rs_recv.at[d, hop, c],
+            send_sem=rs_send.at[stage], recv_sem=rs_recv.at[d, lax.rem(hop, SLOTS), c],
             device_id={"tp": side[d]}, device_id_type=MESH,
         )
 
@@ -93,12 +92,13 @@
     def turn(v, b):
         return v * cosv[b] + pltpu.roll(v, hh, 1) * sinv[b]
 
-    def project(b):
+    def project(b, send=False):
         shared = lax.dot_general(
             tok[b], w_kv[...], (((1,), (1,)), ((), ())), preferred_element_type=jnp.float32
         )
         mine[b] = shared.astype(jnp.bfloat16)
-        pair_copy(b).start()
+        if send:
+            pair_copy(b).start()
         made = jnp.dot(tok[b], wq[...], preferred_element_type=jnp.float32)
         places = (2 * b + s) * rows + lax.broadcasted_iota(jnp.int32, (rows, hd), 0)
         angles = places.astype(jnp.float32) * freq_ref[...]
@@ -174,26 +174,33 @@
                 def _():
                     gather_copy(d, t + 1, came[d], c).start()
 
-            if c == 0:
-
-                @pl.when(t == lag - 1)
-                def _():
-                    assemble(z)
-
-                @pl.when(t >= lag)
-                def _():
-                    assemble(block(lag - 1 - t))
-                    assemble(block(t + 1 - lag))
-
         for b in came:
             project(b)
+
+        @pl.when(t == half - 3)
+        def _():
+            def send_half(k, _):
+                pair_copy(block(k + 2 - half)).start()
+                return 0
+
+            lax.fori_loop(0, 2 * half - 3, send_half, 0)
+
+        @pl.when(t == half - 2)
+        def _():
+            for b in came:
+                pair_copy(b).start()
+
         return 0
 
     lax.fori_loop(0, half - 1, gather_step, 0)
     far = block(half)
-    for u in range(half - 1 - lag, half - 2):
-        assemble(block(-1 - u))
-        assemble(block(1 + u))
+
+    def assemble_shared(k, _):
+        assemble(block(k + 3 - half - parity))
+        return 0
+
+    lax.fori_loop(0, 2 * half - 4, assemble_shared, 0)
+    assemble(block((2 * parity - 1) * (half - 2)))
     assemble(block((1 - 2 * parity) * (half - 1)))
     for c in range(CHUNKS):
         for d in range(2):
@@ -202,7 +209,7 @@
             def _():
                 gather_copy(d, half - 1, far, c).wait_recv()
 
-    project(far)
+    project(far, True)
     assemble(far)
     assemble(block((2 * parity - 1) * (half - 1)))
     cores_kv = whole(kv.at[pl.ds(0, n * rows), :], sp_send.at[0], sp_recv.at[0], {"sp": other})
@@ -293,13 +300,13 @@
             pltpu.VMEM((2, half, CHUNKS, rows, width), bf16),
             dma((5,)),
             dma((1,)),
-            dma((2, half, CHUNKS)),
+            dma((2, SLOTS, CHUNKS)),
             dma((1,)),
             dma((n,)),
             dma((1,)),
             dma((1,)),
             dma((2,)),
-            dma((2, half, CHUNKS)),
+            dma((2, SLOTS, CHUNKS)),
         ],
         compiler_params=pltpu.CompilerParams(
             collective_id=0, has_side_effects=True, vmem_limit_bytes=60 * 1024 * 1024

time: 340 us -> 336 us (0.988)
  Pallas kernels: 338 us -> 334 us
    pallas_call x1, Pallas kernels: 338 us -> 334 us  [layer(): pl.pallas_call(functools.partial(kernel, n, window), out_shape=jax.ShapeD...]
where the time goes in v4:
time: 336 us
  Pallas kernels  334 us (99%)
    pallas_call x1, Pallas kernels, layer(): pl.pallas_call(functools.partial(kernel, n, window), out_shape=jax.ShapeD...  334 us

profile of v4, /device:TPU:37, one launch (start us, length us, event | category | flops | bytes accessed | tf_op | source)
XLA Modules:
  0.0 335.6 jit_solution(14149603498201620701)
XLA Ops:
  0.0 333.8 %shard_map.73 = bf16[48,4608]{1,0:T(8,128)(2,1)} custom-call(bf16[48,4608]{1,0:T(8,128)(2,1)} %x_hbm.1, bf16[4608,128]{1,0:T(8,128)(2,1)} %wq_hbm.1, bf16[64,4608]{1,0:T(8,128)(2,1)} %bitcast.2, bf16[64,4608]{1,0:T(8,128)(2,1)} %bitcast.3, bf16[128,4608]{1,0:T(8,128)(2,1)} %wo_hbm.1, s32[8]{0:T(128)} %lens_ref.1, f32[1,128]{1,0:T(1,128)} %constant.2.clone.freq_ref), custom_call_target="tpu_custom_call" | custom-call | tf_op jit(solution)/shard_map/pallas_call | solution.py:282
  333.8 1.8 copy.9

commit v5 on v4

--- a/solution.py
+++ b/solution.py
@@ -13,7 +13,7 @@
 MASKED = -1e30
 MESH = pl.DeviceIdType.MESH
 CHUNKS = 3
-SLOTS = 4
+SLOTS = 3
 
 
 def kernel(

time: 336 us -> 336 us (level)
  no operation moved by 1% of the time
where the time goes in v5:
time: 336 us
  Pallas kernels  334 us (99%)
    pallas_call x1, Pallas kernels, layer(): pl.pallas_call(functools.partial(kernel, n, window), out_shape=jax.ShapeD...  334 us

profile of v5, /device:TPU:37, one launch (start us, length us, event | category | flops | bytes accessed | tf_op | source)
XLA Modules:
  0.0 335.5 jit_solution(14985010613661775147)
XLA Ops:
  0.0 333.7 %shard_map.73 = bf16[48,4608]{1,0:T(8,128)(2,1)} custom-call(bf16[48,4608]{1,0:T(8,128)(2,1)} %x_hbm.1, bf16[4608,128]{1,0:T(8,128)(2,1)} %wq_hbm.1, bf16[64,4608]{1,0:T(8,128)(2,1)} %bitcast.2, bf16[64,4608]{1,0:T(8,128)(2,1)} %bitcast.3, bf16[128,4608]{1,0:T(8,128)(2,1)} %wo_hbm.1, s32[8]{0:T(128)} %lens_ref.1, f32[1,128]{1,0:T(1,128)} %constant.2.clone.freq_ref), custom_call_target="tpu_custom_call" | custom-call | tf_op jit(solution)/shard_map/pallas_call | solution.py:282
  333.7 1.8 copy.9
